TPU v7x, 32 devices: a whole 2x2x4 slice. The times are simulated.
32 devices in a mesh: rows: 8 (over z, y), cols: 4 (over x, core).
Axes of the slice: x: 2, y: 2, z: 4, core: 2. Of those that a mesh axis runs over, the one named last changes fastest.
Arguments:
- features: bfloat16 [64, 512, 512], P('rows', 'cols'), may hold values from -6 to 6
- dw_weight: float32 [49, 512], replicated, may hold values from -0.875 to 0.875
- norm_gain: float32 [512], replicated, may hold values from 0.1 to 1.9
- w_up: bfloat16 [512, 2048], replicated, may hold values from -0.25 to 0.25
- w_down: bfloat16 [2048, 512], replicated, may hold values from -0.125 to 0.125
- cotangent: bfloat16 [64, 512, 512], P('rows', 'cols'), may hold values from -6 to 6
Outputs:
- grad_input: bfloat16 [64, 512, 512], P('rows', 'cols')
- grad_dw: float32 [49, 512], replicated
- grad_gain: float32 [512], replicated
- grad_up: float32 [512, 2048], replicated
- grad_down: float32 [2048, 512], replicated
All inputs are finite; a program needn't handle non-finite values.
Results may differ from a plain program's by a relative error of at most 0.019.
Values may be sent and summed in bfloat16 or wider, within the bound.
No kernel may reach another device: no remote copies, remote signals or barrier semaphores. Data moves between devices by JAX's collectives and lax.ppermute only.
A program may use at most 128 MiB of HBM per device.

v0:
```python
import jax
import jax.numpy as jnp
from jax import lax
from jax.sharding import PartitionSpec as P

eps = 1e-06


def padded_2(block, sides, width):
    for axis, dim in sides:
        count = lax.axis_size(axis)
        forward = [(i, i + 1) for i in range(count - 1)]
        backward = [(target, source) for source, target in forward]
        low = lax.ppermute(
            lax.slice_in_dim(block, block.shape[dim] - width, None, axis=dim), axis, forward
        )
        high = lax.ppermute(lax.slice_in_dim(block, 0, width, axis=dim), axis, backward)
        block = jnp.concatenate([low, block, high], axis=dim)
    return block


def depthwise(padded, weight, rows, cols):
    total = jnp.zeros((rows, cols, padded.shape[2]), jnp.float32)
    for tap_i in range(7):
        for tap_j in range(7):
            total = (
                total
                + padded[tap_i : tap_i + rows, tap_j : tap_j + cols] * weight[7 * tap_i + tap_j]
            )
    return total


def pointwise(conv, gain, w_up, w_down, grad_out, keep):
    mean = jnp.mean(conv, axis=-1, keepdims=True)
    centred = conv - mean
    inv = lax.rsqrt(jnp.mean(centred * centred, axis=-1, keepdims=True) + eps)
    normed = centred * inv
    scaled = (normed * gain).astype(jnp.bfloat16)
    hidden = jnp.dot(scaled, w_up, preferred_element_type=jnp.float32)
    act = (0.5 * hidden * (1.0 + lax.erf(hidden * 0.7071067811865476))).astype(jnp.bfloat16)
    grad_kept = grad_out * keep.astype(jnp.bfloat16)
    grad_down = lax.dot_general(
        act, grad_kept, (((0,), (0,)), ((), ())), preferred_element_type=jnp.float32
    )
    grad_act = lax.dot_general(
        grad_out, w_down, (((1,), (1,)), ((), ())), preferred_element_type=jnp.float32
    )
    slope = (
        0.5 * (1.0 + lax.erf(hidden * 0.7071067811865476))
        + hidden * jnp.exp(-0.5 * hidden * hidden) * 0.3989422804014327
    )
    grad_hidden = (grad_act * slope).astype(jnp.bfloat16)
    hidden_kept = grad_hidden * keep.astype(jnp.bfloat16)
    grad_up = lax.dot_general(
        scaled, hidden_kept, (((0,), (0,)), ((), ())), preferred_element_type=jnp.float32
    )
    grad_scaled = lax.dot_general(
        grad_hidden, w_up, (((1,), (1,)), ((), ())), preferred_element_type=jnp.float32
    )
    grad_gain = jnp.sum(grad_scaled * normed * keep, axis=0)
    g_norm = grad_scaled * gain
    grad_conv = inv * (
        g_norm
        - jnp.mean(g_norm, axis=-1, keepdims=True)
        - normed * jnp.mean(g_norm * normed, axis=-1, keepdims=True)
    )
    return (grad_conv.astype(jnp.bfloat16), grad_up, grad_down, grad_gain)


def on_device(features, dw_weight, norm_gain, w_up, w_down, cotangent):
    rows, cols, chans = features.shape
    padded = padded_2(features, (("rows", 0), ("cols", 1)), 3).astype(jnp.float32)
    conv = depthwise(padded, dw_weight, rows, cols)
    keep = jnp.ones((rows * cols, 1), jnp.float32)
    grad_flat, grad_up, grad_down, grad_gain = pointwise(
        conv.reshape(rows * cols, chans),
        norm_gain,
        w_up,
        w_down,
        cotangent.reshape(rows * cols, chans),
        keep,
    )
    grad_conv = grad_flat.reshape(rows, cols, chans)
    grad_wide = padded_2(grad_conv, (("rows", 0), ("cols", 1)), 3)
    grad_f = grad_conv.astype(jnp.float32)
    taps = []
    for tap_i in range(7):
        for tap_j in range(7):
            taps.append(
                jnp.sum(padded[tap_i : tap_i + rows, tap_j : tap_j + cols] * grad_f, axis=(0, 1))
            )
    grad_dw = jnp.stack(taps)
    grad_pad = grad_wide.astype(jnp.float32)
    total = cotangent.astype(jnp.float32)
    for tap_i in range(7):
        for tap_j in range(7):
            total = (
                total
                + grad_pad[6 - tap_i : 6 - tap_i + rows, 6 - tap_j : 6 - tap_j + cols]
                * dw_weight[7 * tap_i + tap_j]
            )
    grad_input = total.astype(jnp.bfloat16)
    grad_up, grad_down, grad_dw, grad_gain = lax.psum(
        (grad_up, grad_down, grad_dw, grad_gain), ("rows", "cols")
    )
    return (grad_input, grad_dw, grad_gain, grad_up, grad_down)


def solution(mesh):
    return jax.shard_map(
        on_device,
        mesh=mesh,
        in_specs=(P("rows", "cols", None), P(), P(), P(), P(), P("rows", "cols", None)),
        out_specs=(P("rows", "cols", None), P(), P(), P(), P()),
        check_vma=False,
    )
```

profile of v0, /device:TPU:0, one launch (start us, length us, event | category | flops | bytes accessed | tf_op | source)
XLA Modules:
  0.0 353.4 jit_solution(14381172907683778319)
XLA Ops:
  7.2 0.0 copy-start
  7.2 0.0 copy-start.6
  7.2 0.0 all-reduce.3.cloned.1.call-start
  7.2 1.4 fusion.113
  8.6 4.9 %collective-permute-start = (bf16[3,128,512]{2,1,0:T(8,128)(2,1)S(1)}, bf16[3,128,512]{2,1,0:T(8,128)(2,1)S(1)}, u32[]{:S(2)}, u32[]{:S(2)}) collective-permute-start(bf16[3,128,512]{2,1,0:T(8,128)(2,1)S(1)} %get-tuple-element.70), channel_id=1, source_target_pairs={{0,4},{4,8},{8,12},{12,16},{16,20},{20,24},{24,28},{1,5},{5,9},{9,... | collective-permute-start | bytes 1179656 | tf_op jit(solution)/shard_map/ppermute | solution.py:14
  13.5 1.3 collective-permute-start.1
  14.8 1.1 fusion.114
  16.0 0.0 copy-start.8
  16.0 0.0 copy-start.9
  16.0 0.0 copy-start.10
  16.0 0.0 copy-start.11
  16.1 1.2 fusion.115
  17.5 12.8 %collective-permute-done = bf16[3,128,512]{2,1,0:T(8,128)(2,1)S(1)} collective-permute-done((bf16[3,128,512]{2,1,0:T(8,128)(2,1)S(1)}, bf16[3,128,512]{2,1,0:T(8,128)(2,1)S(1)}, u32[]{:S(2)}, u32[]{:S(2)}) %collective-permute-start) | collective-permute-done | bytes 393248 | tf_op jit(solution)/shard_map/ppermute | solution.py:14
  30.3 0.1 constant_dynamic-update-slice_fusion.1
  30.4 0.0 collective-permute-done.1
  30.5 1.3 collective-permute-start.3
  31.8 3.0 collective-permute-start.2
  34.9 1.6 fusion.116
  36.5 0.0 collective-permute-done.3
  36.5 0.0 collective-permute-done.2
  36.5 2.5 maximum_convert_fusion
  39.1 0.0 copy-done.9
  39.4 54.0 %fusion.110 = (f32[8,128]{1,0:T(8,128)S(1)}, f32[8,128,512]{2,1,0:T(8,128)}) fusion(f32[512]{0:T(512)} %bitcast.48, f32[14,134,512]{2,1,0:T(8,128)} %maximum_convert_fusion, f32[512]{0:T(512)} %bitcast.47, f32[512]{0:T(512)S(1)} %bitcast.183, f32[512]{0:T(512)S(1)} %bitcast.185, f32[512]{0:T(512)S(1)} %bitcast.187, f32[512]{0:T(512)S(1)} %bitcast.189, ...), kind=kLoop, calls=%fused_computation.231 | loop fusion | flops 51379200 | bytes 104962048 | tf_op jit(solution)/shard_map/reduce_sum | solution.py:34
  93.4 0.0 copy-start.2
  93.4 0.0 copy-start.47
  93.4 2.1 multiply_reduce_fusion.2
  95.6 0.0 copy-done.2
  95.6 0.0 copy-done.47
  95.6 0.3 multiply_convert_fusion.3
  96.0 0.0 copy-done
  96.0 0.0 copy-start.4
  96.0 0.0 copy-start.7
  96.0 0.0 copy-start.48
  96.0 2.3 fusion.117
  98.4 5.0 %fusion.5 = bf16[1024,2048]{1,0:T(8,128)(2,1)S(1)} fusion(f32[1024,2048]{1,0:T(8,128)S(1)} %fusion.117, bf16[1024,512]{1,0:T(8,128)(2,1)S(1)} %bitcast.179, bf16[2048,512]{1,0:T(8,128)(2,1)S(1)} %copy-done.48), kind=kOutput, calls=%fused_computation.55 | convolution fusion | flops 2168455168 | bytes 15728640 | tf_op jit(solution)/shard_map/dot_general | solution.py:45
  103.5 0.0 copy-done.49
  103.5 0.0 copy-start.3
  103.5 0.0 copy-start.1
  103.5 3.4 multiply_reduce_fusion
  106.9 0.2 copy-done.1
  107.1 6.6 %fusion.56 = (f32[512]{0:T(512)}, f32[512]{0:T(512)}, f32[512]{0:T(512)}, f32[512]{0:T(512)}, f32[512]{0:T(512)}, /*index=5*/f32[512]{0:T(512)}, f32[512]{0:T(51...) fusion(f32[14,134,512]{2,1,0:T(8,128)S(1)} %copy-done.1, ...), kind=kLoop, calls=%fused_computation.108 | loop fusion | flops 23583744 | bytes 43046912 | tf_op jit(solution)/shard_map/reduce_sum | solution.py:90
  113.7 1.0 fusion.112
  114.7 4.0 %fusion.20 = (f32[512]{0:T(512)}, f32[512]{0:T(512)}, f32[512]{0:T(512)}, f32[512]{0:T(512)}, f32[512]{0:T(512)}, /*index=5*/f32[512]{0:T(512)}, f32[512]{0:T(51...) fusion(f32[14,134,512]{2,1,0:T(8,128)S(1)} %copy-done.1, ...), kind=kLoop, calls=%fused_computation.72 | loop fusion | flops 14149120 | bytes 28338176 | tf_op jit(solution)/shard_map/reduce_sum | solution.py:90
  118.7 5.3 %fusion.38 = (f32[512]{0:T(512)}, f32[512]{0:T(512)}, f32[512]{0:T(512)}, f32[512]{0:T(512)}, f32[512]{0:T(512)}, /*index=5*/f32[512]{0:T(512)}, f32[512]{0:T(51...) fusion(f32[14,134,512]{2,1,0:T(8,128)S(1)} %copy-done.1, ...), kind=kLoop, calls=%fused_computation.90 | loop fusion | flops 19389440 | bytes 38834176 | tf_op jit(solution)/shard_map/reduce_sum | solution.py:90
  124.0 6.1 %fusion.6 = f32[2048,512]{1,0:T(8,128)} fusion(bf16[1024,512]{1,0:T(8,128)(2,1)S(1)} %bitcast.180, f32[1024,2048]{1,0:T(8,128)} %copy-done.49), kind=kOutput, calls=%fused_computation.58 | convolution fusion | flops 2157969408 | bytes 13631488 | tf_op jit(solution)/shard_map/dot_general | solution.py:42
  130.1 1.3 collective-permute-start.5
  131.4 5.8 %collective-permute-start.4 = (bf16[3,128,512]{2,1,0:T(8,128)(2,1)}, bf16[3,128,512]{2,1,0:T(8,128)(2,1)}, u32[]{:S(2)}, u32[]{:S(2)}) collective-permute-start(bf16[3,128,512]{2,1,0:T(8,128)(2,1)} %bitcast.53), channel_id=1, source_target_pairs={{0,4},{4,8},{8,12},{12,16},{16,20},{20,24},{24,28},{1,5},{5,9},{9,... | collective-permute-start | bytes 1179656 | tf_op jit(solution)/shard_map/ppermute | solution.py:14
  137.2 9.4 %stack.199 = f32[49,512]{1,0:T(8,128)} concatenate(f32[1,512]{1,0:T(1,128)} %bitcast.315, f32[1,512]{1,0:T(1,128)} %bitcast.314, f32[1,512]{1,0:T(1,128)} %bitcast.313, f32[1,512]{1,0:T(1,128)} %bitcast.312, f32[1,512]{1,0:T(1,128)} %bitcast.311, f32[1,512]{1,0:T(1,128)} %bitcast.310, f32[1,512]{1,0:T(1,128)} %bitcast.309, f32[1,512]{1,0:T(1,128)} %bitcast.308, ...), dimensions={0} | concatenate | bytes 200704 | tf_op jit(solution)/shard_map/stack | solution.py:92
  146.5 6.9 %fusion.118 = f32[512,2048]{1,0:T(8,128)} fusion(bf16[1024,512]{1,0:T(8,128)(2,1)} %copy-done.4, bf16[1024,2048]{1,0:T(8,128)(2,1)} %copy-done.3), kind=kOutput, calls=%fused_computation.239 | convolution fusion | flops 2147483648 | bytes 9437184 | tf_op jit(solution)/shard_map/dot_general | solution.py:54
  153.4 0.0 all-reduce.3.cloned.1.call-update
  153.5 0.0 collective-permute-done.5
  153.5 0.1 collective-permute-done.4
  153.6 1.4 pad_maximum_fusion.2
  155.1 1.3 collective-permute-start.7
  156.3 3.9 %collective-permute-start.6 = (bf16[14,3,512]{2,1,0:T(4,128)(2,1)}, bf16[14,3,512]{2,1,0:T(4,128)(2,1)}, u32[]{:S(2)}, u32[]{:S(2)}) collective-permute-start(bf16[14,3,512]{2,1,0:T(4,128)(2,1)} %get-tuple-element.63), channel_id=1, source_target_pairs={{0,1},{1,2},{2,3},{4,5},{5,6},{6,7},{8,9},{9,10},{10,11},{12,13},{... | collective-permute-start | bytes 129032 | tf_op jit(solution)/shard_map/ppermute | solution.py:14
  160.2 44.4 %psum.29 = f32[512]{0:T(512)} all-reduce(f32[512]{0:T(512)} %get-tuple-element.54), channel_id=1, replica_groups=mesh['rows'=8,'cols'=4] {'rows','cols'}, use_global_device_ids=true, to_apply=%region_55.0 | all-reduce | flops 512 | bytes 4096 | tf_op jit(solution)/shard_map/psum | solution.py:103
  204.6 0.0 collective-permute-done.7
  204.6 0.0 collective-permute-done.6
  204.6 3.6 %maximum_convert_fusion.1 = f32[14,134,512]{2,1,0:T(8,128)} fusion(bf16[14,3,512]{2,1,0:T(4,128)(2,1)} %collective-permute-done.7, bf16[3,128,512]{2,1,0:T(8,128)(2,1)S(1)} %collective-permute-done.5, bf16[8,128,512]{2,1,0:T(8,128)(2,1)S(1)} %bitcast.178, bf16[3,128,512]{2,1,0:T(8,128)(2,1)} %collective-permute-done.4, ...), kind=kLoop, calls=%fused_computation.217 | loop fusion | flops 9605120 | bytes 5763072 | tf_op jit(solution)/shard_map/convert_element_type | solution.py:93
  208.1 52.3 %fusion.58 = bf16[8,128,512]{2,1,0:T(8,128)(2,1)} fusion(f32[14,134,512]{2,1,0:T(8,128)} %maximum_convert_fusion.1, bf16[8,128,512]{2,1,0:T(8,128)(2,1)} %param.11, f32[512]{0:T(512)} %bitcast.48, f32[512]{0:T(512)} %bitcast.47, f32[512]{0:T(512)S(1)} %bitcast.184, f32[512]{0:T(512)S(1)} %bitcast.186, f32[512]{0:T(512)S(1)} %bitcast.188, f32[512]{0:T(512)} %bitcast.190, ...), kind=kLoop, calls=%fused_computation.111 | loop fusion | flops 52428800 | bytes 104957952 | tf_op jit(solution)/shard_map/convert_element_type | solution.py:102
  260.4 77.8 %all-reduce.3.cloned.1.call-done = (f32[49,512]{1,0:T(8,128)}, f32[512,2048]{1,0:T(8,128)}, f32[2048,512]{1,0:T(8,128)}) async-done(((f32[49,512]{1,0:T(8,128)}, f32[512,2048]{1,0:T(8,128)}, f32[2048,512]{1,0:T(8,128)}), (f32[49,512]{1,0:T(8,128)}, f32[512,2048]{1,0:T(8,128)}, f32[2048,512]{1,0:T(8,128)})) %all-reduce.3.cloned.1.call-update) | async-done | bytes 8488976 | tf_op jit(solution)/shard_map/psum | solution.py:103
  338.2 1.6 copy.16
  339.7 4.8 %copy.17 = f32[512,2048]{1,0:T(8,128)} copy(f32[512,2048]{1,0:T(8,128)} %get-tuple-element.128) | data formatting | bytes 8388608
  344.6 2.0 copy.18
  (87 shorter events, 0.3 us)
Async XLA Ops:
  7.2 88.8 %copy-start = (bf16[512,2048]{1,0:T(8,128)(2,1)S(1)}, bf16[512,2048]{1,0:T(8,128)(2,1)}, u32[]{:S(2)}) copy-start(bf16[512,2048]{1,0:T(8,128)(2,1)} %param.9) | copy-start | bytes 6291460
  7.2 23.1 %copy-start.6 = (bf16[8,128,512]{2,1,0:T(8,128)(2,1)S(1)}, bf16[8,128,512]{2,1,0:T(8,128)(2,1)}, u32[]{:S(2)}) copy-start(bf16[8,128,512]{2,1,0:T(8,128)(2,1)} %param.6) | copy-start | bytes 3145732
  7.2 331.0 %all-reduce.3.cloned.1.call-start = ((), (), s32[]{:S(2)}) async-start(), calls=%async_computation | async-start | bytes 17006592 | tf_op jit(solution)/shard_map/psum | solution.py:103
  8.6 21.7 %collective-permute-start = (bf16[3,128,512]{2,1,0:T(8,128)(2,1)S(1)}, bf16[3,128,512]{2,1,0:T(8,128)(2,1)S(1)}, u32[]{:S(2)}, u32[]{:S(2)}) collective-permute-start(bf16[3,128,512]{2,1,0:T(8,128)(2,1)S(1)} %get-tuple-element.70), channel_id=1, source_target_pairs={{0,4},{4,8},{8,12},{12,16},{16,20},{20,24},{24,28},{1,5},{5,9},{9,... | collective-permute-start | bytes 1179656 | tf_op jit(solution)/shard_map/ppermute | solution.py:14
  13.5 16.9 %collective-permute-start.1 = (bf16[3,128,512]{2,1,0:T(8,128)(2,1)S(1)}, bf16[3,128,512]{2,1,0:T(8,128)(2,1)S(1)}, u32[]{:S(2)}, u32[]{:S(2)}) collective-permute-start(bf16[3,128,512]{2,1,0:T(8,128)(2,1)S(1)} %get-tuple-element.69), channel_id=1, source_target_pairs={{4,0},{8,4},{12,8},{16,12},{20,16},{24,20},{28,24},{5,1},{9,5},{13... | collective-permute-start | bytes 1179656 | tf_op jit(solution)/shard_map/ppermute | solution.py:17
  16.0 23.1 %copy-start.8 = (f32[1,512]{1,0:T(1,128)}, f32[1,512]{1,0:T(1,128)S(1)}, u32[]{:S(2)}) copy-start(f32[1,512]{1,0:T(1,128)S(1)} %get-tuple-element.75) | copy-start | bytes 6148
  16.0 23.1 %copy-start.9 = (f32[1,512]{1,0:T(1,128)}, f32[1,512]{1,0:T(1,128)S(1)}, u32[]{:S(2)}) copy-start(f32[1,512]{1,0:T(1,128)S(1)} %get-tuple-element.76) | copy-start | bytes 6148
  16.0 23.1 %copy-start.10 = (f32[1,512]{1,0:T(1,128)}, f32[1,512]{1,0:T(1,128)S(1)}, u32[]{:S(2)}) copy-start(f32[1,512]{1,0:T(1,128)S(1)} %get-tuple-element.77) | copy-start | bytes 6148
  16.0 23.1 %copy-start.11 = (f32[1,512]{1,0:T(1,128)}, f32[1,512]{1,0:T(1,128)S(1)}, u32[]{:S(2)}) copy-start(f32[1,512]{1,0:T(1,128)S(1)} %get-tuple-element.78) | copy-start | bytes 6148
  16.0 23.1 %copy-start.12 = (f32[1,512]{1,0:T(1,128)}, f32[1,512]{1,0:T(1,128)S(1)}, u32[]{:S(2)}) copy-start(f32[1,512]{1,0:T(1,128)S(1)} %get-tuple-element.79) | copy-start | bytes 6148
  16.0 23.1 %copy-start.13 = (f32[1,512]{1,0:T(1,128)}, f32[1,512]{1,0:T(1,128)S(1)}, u32[]{:S(2)}) copy-start(f32[1,512]{1,0:T(1,128)S(1)} %get-tuple-element.80) | copy-start | bytes 6148
  16.0 23.1 %copy-start.14 = (f32[1,512]{1,0:T(1,128)}, f32[1,512]{1,0:T(1,128)S(1)}, u32[]{:S(2)}) copy-start(f32[1,512]{1,0:T(1,128)S(1)} %get-tuple-element.81) | copy-start | bytes 6148
  16.0 23.1 %copy-start.15 = (f32[1,512]{1,0:T(1,128)}, f32[1,512]{1,0:T(1,128)S(1)}, u32[]{:S(2)}) copy-start(f32[1,512]{1,0:T(1,128)S(1)} %get-tuple-element.82) | copy-start | bytes 6148
  16.0 23.1 %copy-start.16 = (f32[1,512]{1,0:T(1,128)}, f32[1,512]{1,0:T(1,128)S(1)}, u32[]{:S(2)}) copy-start(f32[1,512]{1,0:T(1,128)S(1)} %get-tuple-element.83) | copy-start | bytes 6148
  16.0 23.1 %copy-start.17 = (f32[1,512]{1,0:T(1,128)}, f32[1,512]{1,0:T(1,128)S(1)}, u32[]{:S(2)}) copy-start(f32[1,512]{1,0:T(1,128)S(1)} %get-tuple-element.84) | copy-start | bytes 6148
  16.1 23.1 %copy-start.18 = (f32[1,512]{1,0:T(1,128)}, f32[1,512]{1,0:T(1,128)S(1)}, u32[]{:S(2)}) copy-start(f32[1,512]{1,0:T(1,128)S(1)} %get-tuple-element.85) | copy-start | bytes 6148
  16.1 23.1 %copy-start.19 = (f32[1,512]{1,0:T(1,128)}, f32[1,512]{1,0:T(1,128)S(1)}, u32[]{:S(2)}) copy-start(f32[1,512]{1,0:T(1,128)S(1)} %get-tuple-element.86) | copy-start | bytes 6148
  16.1 23.1 %copy-start.20 = (f32[1,512]{1,0:T(1,128)}, f32[1,512]{1,0:T(1,128)S(1)}, u32[]{:S(2)}) copy-start(f32[1,512]{1,0:T(1,128)S(1)} %get-tuple-element.87) | copy-start | bytes 6148
  16.1 23.1 %copy-start.21 = (f32[1,512]{1,0:T(1,128)}, f32[1,512]{1,0:T(1,128)S(1)}, u32[]{:S(2)}) copy-start(f32[1,512]{1,0:T(1,128)S(1)} %get-tuple-element.88) | copy-start | bytes 6148
  16.1 23.1 %copy-start.22 = (f32[1,512]{1,0:T(1,128)}, f32[1,512]{1,0:T(1,128)S(1)}, u32[]{:S(2)}) copy-start(f32[1,512]{1,0:T(1,128)S(1)} %get-tuple-element.89) | copy-start | bytes 6148
  17.3 21.9 %copy-start.23 = (f32[1,512]{1,0:T(1,128)}, f32[1,512]{1,0:T(1,128)S(1)}, u32[]{:S(2)}) copy-start(f32[1,512]{1,0:T(1,128)S(1)} %get-tuple-element.90) | copy-start | bytes 6148
  17.3 21.9 %copy-start.24 = (f32[1,512]{1,0:T(1,128)}, f32[1,512]{1,0:T(1,128)S(1)}, u32[]{:S(2)}) copy-start(f32[1,512]{1,0:T(1,128)S(1)} %get-tuple-element.91) | copy-start | bytes 6148
  17.3 21.9 %copy-start.25 = (f32[1,512]{1,0:T(1,128)}, f32[1,512]{1,0:T(1,128)S(1)}, u32[]{:S(2)}) copy-start(f32[1,512]{1,0:T(1,128)S(1)} %get-tuple-element.92) | copy-start | bytes 6148
  17.3 21.9 %copy-start.26 = (f32[1,512]{1,0:T(1,128)}, f32[1,512]{1,0:T(1,128)S(1)}, u32[]{:S(2)}) copy-start(f32[1,512]{1,0:T(1,128)S(1)} %get-tuple-element.93) | copy-start | bytes 6148
  17.3 21.9 %copy-start.27 = (f32[1,512]{1,0:T(1,128)}, f32[1,512]{1,0:T(1,128)S(1)}, u32[]{:S(2)}) copy-start(f32[1,512]{1,0:T(1,128)S(1)} %get-tuple-element.94) | copy-start | bytes 6148
  17.3 21.9 %copy-start.28 = (f32[1,512]{1,0:T(1,128)}, f32[1,512]{1,0:T(1,128)S(1)}, u32[]{:S(2)}) copy-start(f32[1,512]{1,0:T(1,128)S(1)} %get-tuple-element.95) | copy-start | bytes 6148
  17.3 21.9 %copy-start.29 = (f32[1,512]{1,0:T(1,128)}, f32[1,512]{1,0:T(1,128)S(1)}, u32[]{:S(2)}) copy-start(f32[1,512]{1,0:T(1,128)S(1)} %get-tuple-element.96) | copy-start | bytes 6148
  17.3 21.9 %copy-start.30 = (f32[1,512]{1,0:T(1,128)}, f32[1,512]{1,0:T(1,128)S(1)}, u32[]{:S(2)}) copy-start(f32[1,512]{1,0:T(1,128)S(1)} %get-tuple-element.97) | copy-start | bytes 6148
  17.4 21.9 %copy-start.31 = (f32[1,512]{1,0:T(1,128)}, f32[1,512]{1,0:T(1,128)S(1)}, u32[]{:S(2)}) copy-start(f32[1,512]{1,0:T(1,128)S(1)} %get-tuple-element.98) | copy-start | bytes 6148
  17.4 21.9 %copy-start.32 = (f32[1,512]{1,0:T(1,128)}, f32[1,512]{1,0:T(1,128)S(1)}, u32[]{:S(2)}) copy-start(f32[1,512]{1,0:T(1,128)S(1)} %get-tuple-element.99) | copy-start | bytes 6148
  17.4 21.9 %copy-start.33 = (f32[1,512]{1,0:T(1,128)}, f32[1,512]{1,0:T(1,128)S(1)}, u32[]{:S(2)}) copy-start(f32[1,512]{1,0:T(1,128)S(1)} %get-tuple-element.100) | copy-start | bytes 6148
  17.4 21.9 %copy-start.34 = (f32[1,512]{1,0:T(1,128)}, f32[1,512]{1,0:T(1,128)S(1)}, u32[]{:S(2)}) copy-start(f32[1,512]{1,0:T(1,128)S(1)} %get-tuple-element.101) | copy-start | bytes 6148
  17.4 21.9 %copy-start.35 = (f32[1,512]{1,0:T(1,128)}, f32[1,512]{1,0:T(1,128)S(1)}, u32[]{:S(2)}) copy-start(f32[1,512]{1,0:T(1,128)S(1)} %get-tuple-element.102) | copy-start | bytes 6148
  17.4 21.9 %copy-start.36 = (f32[1,512]{1,0:T(1,128)}, f32[1,512]{1,0:T(1,128)S(1)}, u32[]{:S(2)}) copy-start(f32[1,512]{1,0:T(1,128)S(1)} %get-tuple-element.103) | copy-start | bytes 6148
  17.4 21.9 %copy-start.37 = (f32[1,512]{1,0:T(1,128)}, f32[1,512]{1,0:T(1,128)S(1)}, u32[]{:S(2)}) copy-start(f32[1,512]{1,0:T(1,128)S(1)} %get-tuple-element.104) | copy-start | bytes 6148
  17.4 21.9 %copy-start.38 = (f32[1,512]{1,0:T(1,128)}, f32[1,512]{1,0:T(1,128)S(1)}, u32[]{:S(2)}) copy-start(f32[1,512]{1,0:T(1,128)S(1)} %get-tuple-element.105) | copy-start | bytes 6148
  17.4 21.9 %copy-start.39 = (f32[1,512]{1,0:T(1,128)}, f32[1,512]{1,0:T(1,128)S(1)}, u32[]{:S(2)}) copy-start(f32[1,512]{1,0:T(1,128)S(1)} %get-tuple-element.106) | copy-start | bytes 6148
  17.4 21.9 %copy-start.40 = (f32[1,512]{1,0:T(1,128)}, f32[1,512]{1,0:T(1,128)S(1)}, u32[]{:S(2)}) copy-start(f32[1,512]{1,0:T(1,128)S(1)} %get-tuple-element.107) | copy-start | bytes 6148
  17.5 21.9 %copy-start.41 = (f32[1,512]{1,0:T(1,128)}, f32[1,512]{1,0:T(1,128)S(1)}, u32[]{:S(2)}) copy-start(f32[1,512]{1,0:T(1,128)S(1)} %get-tuple-element.108) | copy-start | bytes 6148
  30.5 6.0 %collective-permute-start.3 = (bf16[14,3,512]{2,1,0:T(4,128)(2,1)S(1)}, bf16[14,3,512]{2,1,0:T(4,128)(2,1)S(1)}, u32[]{:S(2)}, u32[]{:S(2)}) collective-permute-start(bf16[14,3,512]{2,1,0:T(4,128)(2,1)S(1)} %get-tuple-element.66), channel_id=1, source_target_pairs={{1,0},{2,1},{3,2},{5,4},{6,5},{7,6},{9,8},{10,9},{11,10},{13,12},{... | collective-permute-start | bytes 129032 | tf_op jit(solution)/shard_map/ppermute | solution.py:17
  31.8 4.7 %collective-permute-start.2 = (bf16[14,3,512]{2,1,0:T(4,128)(2,1)S(1)}, bf16[14,3,512]{2,1,0:T(4,128)(2,1)S(1)}, u32[]{:S(2)}, u32[]{:S(2)}) collective-permute-start(bf16[14,3,512]{2,1,0:T(4,128)(2,1)S(1)} %get-tuple-element.65), channel_id=1, source_target_pairs={{0,1},{1,2},{2,3},{4,5},{5,6},{6,7},{8,9},{9,10},{10,11},{12,13},{... | collective-permute-start | bytes 129032 | tf_op jit(solution)/shard_map/ppermute | solution.py:14
  36.5 2.9 copy-start.42
  36.5 2.9 copy-start.43
  36.5 2.9 copy-start.44
  36.5 2.9 copy-start.45
  36.5 2.9 copy-start.46
  93.4 2.2 copy-start.2
  93.4 2.2 copy-start.47
  96.0 2.4 copy-start.4
  96.0 2.4 copy-start.7
  96.0 2.4 copy-start.48
  98.4 5.1 %copy-start.49 = (f32[1024,2048]{1,0:T(8,128)}, f32[1024,2048]{1,0:T(8,128)S(1)}, u32[]{:S(2)}) copy-start(f32[1024,2048]{1,0:T(8,128)S(1)} %fusion.117) | copy-start | bytes 25165828
  103.5 3.4 copy-start.3
  103.5 3.6 %copy-start.1 = (f32[14,134,512]{2,1,0:T(8,128)S(1)}, f32[14,134,512]{2,1,0:T(8,128)}, u32[]{:S(2)}) copy-start(f32[14,134,512]{2,1,0:T(8,128)} %maximum_convert_fusion) | copy-start | bytes 11526148
  130.1 23.3 %collective-permute-start.5 = (bf16[3,128,512]{2,1,0:T(8,128)(2,1)}, bf16[3,128,512]{2,1,0:T(8,128)(2,1)S(1)}, u32[]{:S(2)}, u32[]{:S(2)}) collective-permute-start(bf16[3,128,512]{2,1,0:T(8,128)(2,1)} %bitcast.55), channel_id=1, source_target_pairs={{4,0},{8,4},{12,8},{16,12},{20,16},{24,20},{28,24},{5,1},{9,5},{13... | collective-permute-start | bytes 1179656 | tf_op jit(solution)/shard_map/ppermute | solution.py:17
  131.4 22.2 %collective-permute-start.4 = (bf16[3,128,512]{2,1,0:T(8,128)(2,1)}, bf16[3,128,512]{2,1,0:T(8,128)(2,1)}, u32[]{:S(2)}, u32[]{:S(2)}) collective-permute-start(bf16[3,128,512]{2,1,0:T(8,128)(2,1)} %bitcast.53), channel_id=1, source_target_pairs={{0,4},{4,8},{8,12},{12,16},{16,20},{20,24},{24,28},{1,5},{5,9},{9,... | collective-permute-start | bytes 1179656 | tf_op jit(solution)/shard_map/ppermute | solution.py:14
  155.1 49.5 %collective-permute-start.7 = (bf16[14,3,512]{2,1,0:T(4,128)(2,1)}, bf16[14,3,512]{2,1,0:T(4,128)(2,1)}, u32[]{:S(2)}, u32[]{:S(2)}) collective-permute-start(bf16[14,3,512]{2,1,0:T(4,128)(2,1)} %get-tuple-element.64), channel_id=1, source_target_pairs={{1,0},{2,1},{3,2},{5,4},{6,5},{7,6},{9,8},{10,9},{11,10},{13,12},{... | collective-permute-start | bytes 129032 | tf_op jit(solution)/shard_map/ppermute | solution.py:17
  156.3 48.2 %collective-permute-start.6 = (bf16[14,3,512]{2,1,0:T(4,128)(2,1)}, bf16[14,3,512]{2,1,0:T(4,128)(2,1)}, u32[]{:S(2)}, u32[]{:S(2)}) collective-permute-start(bf16[14,3,512]{2,1,0:T(4,128)(2,1)} %get-tuple-element.63), channel_id=1, source_target_pairs={{0,1},{1,2},{2,3},{4,5},{5,6},{6,7},{8,9},{9,10},{10,11},{12,13},{... | collective-permute-start | bytes 129032 | tf_op jit(solution)/shard_map/ppermute | solution.py:14
  339.7 4.9 %copy-start.5 = (f32[2048,512]{1,0:T(8,128)S(1)}, f32[2048,512]{1,0:T(8,128)}, u32[]{:S(2)}) copy-start(f32[2048,512]{1,0:T(8,128)} %get-tuple-element.129) | copy-start | bytes 12582916
Sparse Core Ops, SparseCore 0:
  153.6 184.5 all-reduce.2
where the time goes:
time: 354 us; the launch traced here: 353 us
  other arithmetic  132 us (37%)
  waiting for transfers between devices  90.8 us (26%)
  blocking collectives  44.4 us (13%)
  local copies, waits for them, and re-layouts  24.7 us (7%)
  matrix products  23.8 us (7%)
  starting transfers between devices  22.8 us (6%)
  between operations  14.9 us (4%)
    psum x1, waiting for transfers between devices, on_device(): lax.psum((grad_up, grad_down, grad_dw, grad_gain), ('rows', 'cols'))  77.8 us
    reduce_sum x1, other arithmetic, pointwise(): mean = jnp.mean(conv, axis=-1, keepdims=True)  54 us
    convert_element_type x1, other arithmetic, on_device(): grad_input = total.astype(jnp.bfloat16)  52.3 us
    psum x1, blocking collectives, on_device(): lax.psum((grad_up, grad_down, grad_dw, grad_gain), ('rows', 'cols'))  44.4 us
    ppermute x4, starting transfers between devices, padded_2(): lax.ppermute(lax.slice_in_dim(block, block.shape[dim] - width, None, axis...  17.6 us
    reduce_sum x3, other arithmetic, on_device(): jnp.sum(padded[tap_i:tap_i + rows, tap_j:tap_j + cols] * grad_f, axis=(0,...  15.9 us
    ppermute x4, waiting for transfers between devices, padded_2(): lax.ppermute(lax.slice_in_dim(block, block.shape[dim] - width, None, axis...  13 us
    another operation x1, local copies, waits for them, and re-layouts, on_device(): grad_dw = jnp.stack(taps)  9.36 us
  transfers between devices with their start and end apart: 9, of which 3 were waited for; matrix products, arithmetic and copies ran while one was open for 22% of the time, Pallas kernels for 0%

commit v1 on v0

--- a/solution.py
+++ b/solution.py
@@ -101,7 +101,7 @@
             )
     grad_input = total.astype(jnp.bfloat16)
     grad_up, grad_down, grad_dw, grad_gain = lax.psum(
-        (grad_up, grad_down, grad_dw, grad_gain), ("rows", "cols")
+        lax.psum((grad_up, grad_down, grad_dw, grad_gain), "cols"), "rows"
     )
     return (grad_input, grad_dw, grad_gain, grad_up, grad_down)
 

time: 354 us -> 595 us (1.68)
  waiting for transfers between devices: 90.8 us -> 360 us
  blocking collectives: 44.4 us -> 28.7 us
    psum x1 -> x2, waiting for transfers between devices: 77.8 us -> 323 us  [the longest x1 164 us: on_device(): lax.psum(lax.psum((grad_up, grad_down, grad_dw, grad_gain), 'cols'), 'rows')]
    ppermute x4, waiting for transfers between devices: 13 us -> 29 us  [padded_2(): lax.ppermute(lax.slice_in_dim(block, block.shape[dim] - width, None, axis...]
    psum x1 -> x2, blocking collectives: 44.4 us -> 28.7 us  [the longest x1 21.5 us: on_device(): lax.psum(lax.psum((grad_up, grad_down, grad_dw, grad_gain), 'cols'), 'rows')]
    ppermute x4, waiting for transfers between devices: 0.01 us -> 7.6 us  [padded_2(): lax.ppermute(lax.slice_in_dim(block, 0, width, axis=dim), axis, backward)]
  transfers between devices with their start and end apart: 9 -> 10, of which waited for: 3 -> 5; matrix products, arithmetic and copies ran while one was open for 22% -> 10% of each run, Pallas kernels for 0% -> 0%
where the time goes in v1:
time: 595 us; the launch traced here: 594 us
  waiting for transfers between devices  360 us (61%)
  other arithmetic  131 us (22%)
  blocking collectives  28.7 us (5%)
  matrix products  20.9 us (4%)
  starting transfers between devices  20.8 us (3%)
  local copies, waits for them, and re-layouts  18.9 us (3%)
  between operations  14.4 us (2%)
    psum x1, waiting for transfers between devices, on_device(): lax.psum(lax.psum((grad_up, grad_down, grad_dw, grad_gain), 'cols'), 'rows')  164 us
    psum x1, waiting for transfers between devices, on_device(): lax.psum((grad_up, grad_down, grad_dw, grad_gain), 'cols')  159 us
    reduce_sum x1, other arithmetic, pointwise(): mean = jnp.mean(conv, axis=-1, keepdims=True)  55.9 us
    convert_element_type x1, other arithmetic, on_device(): grad_input = total.astype(jnp.bfloat16)  52.9 us
    ppermute x4, waiting for transfers between devices, padded_2(): lax.ppermute(lax.slice_in_dim(block, block.shape[dim] - width, None, axis...  29 us
    psum x1, blocking collectives, on_device(): lax.psum(lax.psum((grad_up, grad_down, grad_dw, grad_gain), 'cols'), 'rows')  21.5 us
    ppermute x4, starting transfers between devices, padded_2(): lax.ppermute(lax.slice_in_dim(block, block.shape[dim] - width, None, axis...  15.6 us
    reduce_sum x3, other arithmetic, on_device(): jnp.sum(padded[tap_i:tap_i + rows, tap_j:tap_j + cols] * grad_f, axis=(0,...  14.3 us
  transfers between devices with their start and end apart: 10, of which 5 were waited for; matrix products, arithmetic and copies ran while one was open for 10% of the time, Pallas kernels for 0%

profile of v1, /device:TPU:0, one launch (start us, length us, event | category | flops | bytes accessed | tf_op | source)
XLA Modules:
  0.0 594.0 jit_solution(7654602855492389848)
XLA Ops:
  7.2 0.0 copy-start
  7.2 0.0 copy-start.5
  7.2 0.0 all-reduce.7.cloned.1.call-start
  7.2 1.4 fusion.113
  8.6 4.9 collective-permute-start
  13.5 1.3 collective-permute-start.1
  14.8 1.1 fusion.114
  15.9 1.2 fusion.115
  17.1 13.2 %collective-permute-done = bf16[3,128,512]{2,1,0:T(8,128)(2,1)S(1)} collective-permute-done((bf16[3,128,512]{2,1,0:T(8,128)(2,1)S(1)}, bf16[3,128,512]{2,1,0:T(8,128)(2,1)S(1)}, u32[]{:S(2)}, u32[]{:S(2)}) %collective-permute-start) | collective-permute-done | bytes 393248 | tf_op jit(solution)/shard_map/ppermute | solution.py:14
  30.3 0.0 copy-done.5
  30.3 0.1 constant_dynamic-update-slice_fusion.1
  30.4 0.0 collective-permute-done.1
  30.6 1.3 collective-permute-start.3
  31.9 3.0 collective-permute-start.2
  34.9 1.0 fusion.116
  35.9 0.0 collective-permute-done.3
  35.9 0.0 collective-permute-done.2
  35.9 2.5 maximum_convert_fusion
  38.4 55.9 %fusion.110 = (f32[8,128]{1,0:T(8,128)S(1)}, f32[8,128,512]{2,1,0:T(8,128)}) fusion(f32[512]{0:T(512)S(1)} %bitcast.277, f32[14,134,512]{2,1,0:T(8,128)} %maximum_convert_fusion, f32[512]{0:T(512)S(1)} %bitcast.279, f32[512]{0:T(512)S(1)} %bitcast.185, f32[512]{0:T(512)S(1)} %bitcast.187, f32[512]{0:T(512)S(1)} %bitcast.189, f32[512]{0:T(512)S(1)} %bitcast.191, ...), kind=kLoop, calls=%fused_computation.231 | loop fusion | flops 51379200 | bytes 104962048 | tf_op jit(solution)/shard_map/reduce_sum | solution.py:34
  94.3 0.0 copy-start.3
  94.3 0.0 copy-start.7
  94.3 2.1 multiply_reduce_fusion.2
  96.5 0.0 copy-done.3
  96.5 0.0 copy-done.7
  96.5 0.3 multiply_convert_fusion.3
  96.9 0.0 copy-done
  96.9 0.0 copy-start.6
  96.9 0.0 copy-start.8
  96.9 2.3 fusion.117
  99.3 0.0 copy-start.9
  99.3 0.0 copy-done.6
  99.3 0.0 copy-done.8
  99.3 5.0 fusion.5
  104.4 0.0 copy-start.2
  104.4 2.9 multiply_reduce_fusion
  107.2 0.0 copy-done.2
  107.2 6.2 %fusion.56 = (f32[512]{0:T(512)S(1)}, f32[512]{0:T(512)S(1)}, f32[512]{0:T(512)S(1)}, f32[512]{0:T(512)S(1)}, f32[512]{0:T(512)S(1)}, /*index=5*/f32[512]{0:T(51...) fusion(f32[14,134,512]{2,1,0:T(8,128)S(1)} %copy-done.2, ...), kind=kLoop, calls=%fused_computation.108 | loop fusion | flops 23583744 | bytes 43046912 | tf_op jit(solution)/shard_map/reduce_sum | solution.py:90
  113.5 3.4 fusion.20
  116.9 4.7 fusion.38
  121.5 4.5 fusion.118
  126.0 6.2 %fusion.6 = f32[2048,512]{1,0:T(8,128)} fusion(bf16[1024,512]{1,0:T(8,128)(2,1)S(1)} %bitcast.180, f32[1024,2048]{1,0:T(8,128)} %copy-done.9), kind=kOutput, calls=%fused_computation.58 | convolution fusion | flops 2157969408 | bytes 13631488 | tf_op jit(solution)/shard_map/dot_general | solution.py:42
  132.2 4.4 stack.199
  136.6 0.0 all-reduce.7.cloned.1.call-update
  136.6 0.0 all-reduce.5.cloned.1.call-start
  136.7 159.3 %all-reduce.7.cloned.1.call-done = (f32[49,512]{1,0:T(8,128)}, f32[512,2048]{1,0:T(8,128)}, f32[2048,512]{1,0:T(8,128)}) async-done(((f32[49,512]{1,0:T(8,128)}, f32[512,2048]{1,0:T(8,128)}, f32[2048,512]{1,0:T(8,128)}), (f32[49,512]{1,0:T(8,128)}, f32[512,2048]{1,0:T(8,128)}, f32[2048,512]{1,0:T(8,128)})) %all-reduce.7.cloned.1.call-update) | async-done | bytes 8488976 | tf_op jit(solution)/shard_map/psum | solution.py:104
  295.9 0.0 all-reduce.5.cloned.1.call-update
  296.0 0.1 fusion.112
  296.0 1.3 collective-permute-start.5
  297.3 4.6 collective-permute-start.4
  301.9 7.6 %collective-permute-done.5 = bf16[3,128,512]{2,1,0:T(8,128)(2,1)S(1)} collective-permute-done((bf16[3,128,512]{2,1,0:T(8,128)(2,1)S(1)}, bf16[3,128,512]{2,1,0:T(8,128)(2,1)S(1)}, u32[]{:S(2)}, u32[]{:S(2)}) %collective-permute-start.5) | collective-permute-done | bytes 393248 | tf_op jit(solution)/shard_map/ppermute | solution.py:17
  309.5 15.8 %collective-permute-done.4 = bf16[3,128,512]{2,1,0:T(8,128)(2,1)S(1)} collective-permute-done((bf16[3,128,512]{2,1,0:T(8,128)(2,1)S(1)}, bf16[3,128,512]{2,1,0:T(8,128)(2,1)S(1)}, u32[]{:S(2)}, u32[]{:S(2)}) %collective-permute-start.4) | collective-permute-done | bytes 393248 | tf_op jit(solution)/shard_map/ppermute | solution.py:14
  325.3 1.3 collective-permute-start.7
  326.6 3.0 collective-permute-start.6
  329.7 7.1 %psum.58 = f32[512]{0:T(512)S(1)} all-reduce(f32[512]{0:T(512)S(1)} %get-tuple-element.54), channel_id=1, replica_groups=mesh['rows'=8,'cols'=4] {'cols'}, use_global_device_ids=true, to_apply=%region_56.0 | all-reduce | flops 512 | bytes 4096 | tf_op jit(solution)/shard_map/psum | solution.py:104
  336.8 21.5 %psum.59 = f32[512]{0:T(512)} all-reduce(f32[512]{0:T(512)S(1)} %psum.58), channel_id=1, replica_groups=mesh['rows'=8,'cols'=4] {'rows'}, use_global_device_ids=true, to_apply=%region_57.0 | all-reduce | flops 512 | bytes 4096 | tf_op jit(solution)/shard_map/psum | solution.py:103
  358.3 0.0 collective-permute-done.7
  358.3 0.0 collective-permute-done.6
  358.3 2.5 maximum_convert_fusion.1
  360.9 52.9 %fusion.58 = bf16[8,128,512]{2,1,0:T(8,128)(2,1)} fusion(f32[14,134,512]{2,1,0:T(8,128)} %maximum_convert_fusion.1, bf16[8,128,512]{2,1,0:T(8,128)(2,1)S(1)} %copy-done.6, f32[512]{0:T(512)S(1)} %bitcast.278, f32[512]{0:T(512)S(1)} %bitcast.280, f32[512]{0:T(512)S(1)} %bitcast.186, f32[512]{0:T(512)S(1)} %bitcast.188, f32[512]{0:T(512)S(1)} %bitcast.190, ...), kind=kLoop, calls=%fused_computation.111 | loop fusion | flops 52428800 | bytes 104957952 | tf_op jit(solution)/shard_map/convert_element_type | solution.py:102
  413.7 163.9 %all-reduce.5.cloned.1.call-done = (f32[49,512]{1,0:T(8,128)}, f32[512,2048]{1,0:T(8,128)}, f32[2048,512]{1,0:T(8,128)}) async-done(((f32[49,512]{1,0:T(8,128)}, f32[512,2048]{1,0:T(8,128)}, f32[2048,512]{1,0:T(8,128)}), (f32[49,512]{1,0:T(8,128)}, f32[512,2048]{1,0:T(8,128)}, f32[2048,512]{1,0:T(8,128)})) %all-reduce.5.cloned.1.call-update) | async-done | bytes 8488976 | tf_op jit(solution)/shard_map/psum | solution.py:103
  577.7 1.6 copy.19
  579.2 4.8 copy.20
  584.1 2.1 copy.21
  586.2 1.0 copy-done.1
  (11 shorter events, 0.2 us)
Async XLA Ops:
  7.2 89.7 %copy-start = (bf16[512,2048]{1,0:T(8,128)(2,1)S(1)}, bf16[512,2048]{1,0:T(8,128)(2,1)}, u32[]{:S(2)}) copy-start(bf16[512,2048]{1,0:T(8,128)(2,1)} %param.9) | copy-start | bytes 6291460
  7.2 23.1 %copy-start.5 = (bf16[8,128,512]{2,1,0:T(8,128)(2,1)S(1)}, bf16[8,128,512]{2,1,0:T(8,128)(2,1)}, u32[]{:S(2)}) copy-start(bf16[8,128,512]{2,1,0:T(8,128)(2,1)} %param.6) | copy-start | bytes 3145732
  7.2 288.8 %all-reduce.7.cloned.1.call-start = ((), (), s32[]{:S(2)}) async-start(), calls=%async_computation.1 | async-start | bytes 17006592 | tf_op jit(solution)/shard_map/psum | solution.py:104
  8.6 21.7 %collective-permute-start = (bf16[3,128,512]{2,1,0:T(8,128)(2,1)S(1)}, bf16[3,128,512]{2,1,0:T(8,128)(2,1)S(1)}, u32[]{:S(2)}, u32[]{:S(2)}) collective-permute-start(bf16[3,128,512]{2,1,0:T(8,128)(2,1)S(1)} %get-tuple-element.73), channel_id=1, source_target_pairs={{0,4},{4,8},{8,12},{12,16},{16,20},{20,24},{24,28},{1,5},{5,9},{9,... | collective-permute-start | bytes 1179656 | tf_op jit(solution)/shard_map/ppermute | solution.py:14
  13.5 16.9 %collective-permute-start.1 = (bf16[3,128,512]{2,1,0:T(8,128)(2,1)S(1)}, bf16[3,128,512]{2,1,0:T(8,128)(2,1)S(1)}, u32[]{:S(2)}, u32[]{:S(2)}) collective-permute-start(bf16[3,128,512]{2,1,0:T(8,128)(2,1)S(1)} %get-tuple-element.72), channel_id=1, source_target_pairs={{4,0},{8,4},{12,8},{16,12},{20,16},{24,20},{28,24},{5,1},{9,5},{13... | collective-permute-start | bytes 1179656 | tf_op jit(solution)/shard_map/ppermute | solution.py:17
  30.6 5.3 collective-permute-start.3
  31.9 4.0 collective-permute-start.2
  94.3 2.2 copy-start.3
  94.3 2.2 copy-start.7
  96.9 2.4 copy-start.6
  96.9 2.4 copy-start.8
  99.3 5.1 copy-start.9
  104.4 2.9 copy-start.2
  136.6 441.0 %all-reduce.5.cloned.1.call-start = ((), (), s32[]{:S(2)}) async-start(), calls=%async_computation | async-start | bytes 17006592 | tf_op jit(solution)/shard_map/psum | solution.py:103
  296.0 13.5 %collective-permute-start.5 = (bf16[3,128,512]{2,1,0:T(8,128)(2,1)S(1)}, bf16[3,128,512]{2,1,0:T(8,128)(2,1)S(1)}, u32[]{:S(2)}, u32[]{:S(2)}) collective-permute-start(bf16[3,128,512]{2,1,0:T(8,128)(2,1)S(1)} %bitcast.182), channel_id=1, source_target_pairs={{4,0},{8,4},{12,8},{16,12},{20,16},{24,20},{28,24},{5,1},{9,5},{13... | collective-permute-start | bytes 1179656 | tf_op jit(solution)/shard_map/ppermute | solution.py:17
  297.3 28.0 %collective-permute-start.4 = (bf16[3,128,512]{2,1,0:T(8,128)(2,1)S(1)}, bf16[3,128,512]{2,1,0:T(8,128)(2,1)S(1)}, u32[]{:S(2)}, u32[]{:S(2)}) collective-permute-start(bf16[3,128,512]{2,1,0:T(8,128)(2,1)S(1)} %bitcast.181), channel_id=1, source_target_pairs={{0,4},{4,8},{8,12},{12,16},{16,20},{20,24},{24,28},{1,5},{5,9},{9,... | collective-permute-start | bytes 1179656 | tf_op jit(solution)/shard_map/ppermute | solution.py:14
  325.3 33.0 %collective-permute-start.7 = (bf16[14,3,512]{2,1,0:T(4,128)(2,1)S(1)}, bf16[14,3,512]{2,1,0:T(4,128)(2,1)S(1)}, u32[]{:S(2)}, u32[]{:S(2)}) collective-permute-start(bf16[14,3,512]{2,1,0:T(4,128)(2,1)S(1)} %get-tuple-element.67), channel_id=1, source_target_pairs={{1,0},{2,1},{3,2},{5,4},{6,5},{7,6},{9,8},{10,9},{11,10},{13,12},{... | collective-permute-start | bytes 129032 | tf_op jit(solution)/shard_map/ppermute | solution.py:17
  326.6 31.7 %collective-permute-start.6 = (bf16[14,3,512]{2,1,0:T(4,128)(2,1)S(1)}, bf16[14,3,512]{2,1,0:T(4,128)(2,1)S(1)}, u32[]{:S(2)}, u32[]{:S(2)}) collective-permute-start(bf16[14,3,512]{2,1,0:T(4,128)(2,1)S(1)} %get-tuple-element.66), channel_id=1, source_target_pairs={{0,1},{1,2},{2,3},{4,5},{5,6},{6,7},{8,9},{9,10},{10,11},{12,13},{... | collective-permute-start | bytes 129032 | tf_op jit(solution)/shard_map/ppermute | solution.py:14
  579.2 4.9 copy-start.4
  584.1 3.1 copy-start.1
Sparse Core Ops, SparseCore 0:
  136.8 159.1 all-reduce.6
  300.5 277.1 all-reduce.4
